TPU v7x, 32 devices: a whole 2x2x4 slice. The times are simulated.
32 devices in a mesh: gx: 4 (over y, x), gy: 8 (over z, core).
Axes of the slice: x: 2, y: 2, z: 4, core: 2. Of those that a mesh axis runs over, the one named last changes fastest.
Arguments:
- expert_grad: bfloat16 [8, 512, 14336], P('gx', None, 'gy'), may hold values from -40000 to 40000
- attn_grad: bfloat16 [4, 2048, 4096], P('gx', None, 'gy'), may hold values from -40000 to 40000
- expert_master: float32 [4096, 14336], P(('gx', 'gy')), may hold values from -0.75 to 0.75
- expert_moment: float32 [4096, 14336], P(('gx', 'gy')), may hold values from -6 to 6
- expert_second: float32 [4096, 14336], P(('gx', 'gy')), may hold values from 0.1 to 4
- attn_master: float32 [2048, 4096], P(('gx', 'gy')), may hold values from -0.75 to 0.75
- attn_moment: float32 [2048, 4096], P(('gx', 'gy')), may hold values from -6 to 6
- attn_second: float32 [2048, 4096], P(('gx', 'gy')), may hold values from 0.1 to 4
Outputs:
- expert_master_new: float32 [4096, 14336], P(('gx', 'gy'))
- expert_moment_new: float32 [4096, 14336], P(('gx', 'gy'))
- expert_second_new: float32 [4096, 14336], P(('gx', 'gy'))
- attn_master_new: float32 [2048, 4096], P(('gx', 'gy'))
- attn_moment_new: float32 [2048, 4096], P(('gx', 'gy'))
- attn_second_new: float32 [2048, 4096], P(('gx', 'gy'))
- expert_weight: bfloat16 [8, 512, 14336], P('gx', None, 'gy')
- attn_weight: bfloat16 [2048, 4096], P(None, 'gy')
All inputs are finite; a program needn't handle non-finite values.
Results may differ from a plain program's by a relative error of at most 0.001.
Values may be sent and summed in bfloat16 or wider, within the bound.
A program may use at most 128 MiB of HBM per device.

v0:
```python
import functools
import math

import jax
import jax.numpy as jnp
from jax import lax
from jax.experimental import pallas as pl
from jax.experimental.pallas import tpu as pltpu
from jax.sharding import PartitionSpec as P

MESH = pl.DeviceIdType.MESH

beta_one = 0.9
beta_two = 0.95
learn_rate = 0.01
weight_decay = 0.1
adam_eps = 1e-08
bias_one = 1.0 - 0.9**20
bias_two = 1.0 - 0.95**20


def adam_update(gradient, master, moment, second, clip_factor):
    scaled = clip_factor * gradient
    moment_new = beta_one * moment + (1.0 - beta_one) * scaled
    second_new = beta_two * second + (1.0 - beta_two) * scaled * scaled
    update = moment_new / bias_one / (jnp.sqrt(second_new / bias_two) + adam_eps)
    master_new = master - learn_rate * (update + weight_decay * master)
    return (master_new, moment_new, second_new)


def partner_to(me, k, n):
    if n & (n - 1):
        return lax.rem(me + k, n)
    out, bit = me, 1
    while bit < n:
        if k & bit:
            out = out + bit * (1 - 2 * lax.rem(me // bit, 2))
        bit *= 2
    return out


def partner_from(me, k, n):
    if n & (n - 1):
        return lax.rem(me + n - k, n)
    return partner_to(me, k, n)


def send_order(n):
    return list(range(n - 1, 0, -1))


def col_chunk(width):
    return 256 if width % 256 == 0 else 128


def row_chunk(rows):
    return math.gcd(rows, 16)


def step_kernel(
    n_out, n_in, numel,
    eg, ag, em, eo, es, am, ao, as_,
    em_o, eo_o, es_o, am_o, ao_o, as_o, ew_o, aw_o,
    mine, held, arep, asum, agot, aback, part, acc,
    own_sem, state_sem, f_send, f_recv, g_send, g_recv, h_send, h_recv,
    p_send, p_recv, q_send, q_recv, r_send, r_recv, s_send, s_recv, t_send, t_recv,
):
    out_me = lax.axis_index("gx")
    in_me = lax.axis_index("gy")
    rows, width = held.shape[1], held.shape[2]
    block_rows, a_width = arep.shape[1], arep.shape[2]
    a_rows = agot.shape[1]

    def to_in(k):
        return (out_me, partner_to(in_me, k, n_in))

    def to_out(k):
        return (partner_to(out_me, k, n_out), in_me)

    def remote(src, dst, send, recv, where):
        return pltpu.make_async_remote_copy(
            src_ref=src, dst_ref=dst, send_sem=send, recv_sem=recv,
            device_id=where, device_id_type=MESH,
        )

    def rows_at(ref, index, count):
        return ref.at[pl.ds(pl.multiple_of(index * count, count), count)]

    barrier = pltpu.get_barrier_semaphore()
    for k in range(1, n_in):
        pl.semaphore_signal(barrier, inc=1, device_id=to_in(k), device_id_type=MESH)
    for k in range(1, n_out):
        pl.semaphore_signal(barrier, inc=1, device_id=to_out(k), device_id_type=MESH)

    load_grad = pltpu.make_async_copy(eg, mine, own_sem.at[0])
    load_grad.start()
    load_rep = pltpu.make_async_copy(rows_at(ag, out_me, block_rows), arep.at[0], own_sem.at[1])
    load_rep.start()
    pl.semaphore_wait(barrier, n_in - 1 + n_out - 1)

    rep_copies = {}
    for k in send_order(n_out):
        c = remote(
            rows_at(ag, partner_to(out_me, k, n_out), block_rows), arep.at[k],
            g_send.at[k], g_recv.at[k], to_out(k),
        )
        c.start()
        rep_copies[k] = c
    order = send_order(n_in)
    far, near = order[: n_in // 2], order[n_in // 2 :]
    first = far[: n_in // 4] + near[:1]
    rest = near[1:] + far[n_in // 4 :]
    arrival = first + near[1:] + [0] + far[n_in // 4 :]
    fwd = {}

    def send_fwd(k):
        c = remote(
            rows_at(eg, partner_to(in_me, k, n_in), rows), held.at[k],
            f_send.at[k], f_recv.at[k], to_in(k),
        )
        c.start()
        fwd[k] = c

    for k in first:
        send_fwd(k)

    state = []
    for i, (src, dst) in enumerate(
        ((em, em_o), (eo, eo_o), (es, es_o), (am, am_o), (ao, ao_o), (as_, as_o))
    ):
        c = pltpu.make_async_copy(src, dst, state_sem.at[i])
        c.start()
        state.append(c)

    load_grad.wait()
    chunk = col_chunk(width)
    rc = row_chunk(mine.shape[0])

    def square_rows(i, carry):
        r = pl.ds(pl.multiple_of(i * rc, rc), rc)
        for c in range(width // chunk):
            x = mine[r, c * chunk : (c + 1) * chunk].astype(jnp.float32)
            carry = carry + x * x
        return carry

    e_sq = lax.fori_loop(0, mine.shape[0] // rc, square_rows, jnp.zeros((rc, chunk), jnp.float32))

    load_rep.wait()
    for k in send_order(n_out):
        rep_copies[k].wait_recv()
    a_chunk = col_chunk(a_width)
    arc = row_chunk(block_rows)

    def sum_rows(i, carry):
        r = pl.ds(pl.multiple_of(i * arc, arc), arc)
        for c in range(a_width // a_chunk):
            cols = slice(c * a_chunk, (c + 1) * a_chunk)
            x = arep[0, r, cols].astype(jnp.float32)
            for k in range(1, n_out):
                x = x + arep[k, r, cols].astype(jnp.float32)
            asum[r, cols] = x
            carry = carry + x * x
        return carry

    a_sq = lax.fori_loop(0, block_rows // arc, sum_rows, jnp.zeros((arc, a_chunk), jnp.float32))
    total = jnp.sum(e_sq) + jnp.sum(a_sq)
    part[0] = jnp.full(part.shape[1:], total, jnp.float32)

    own_rows = pltpu.make_async_copy(rows_at(asum, in_me, a_rows), agot.at[0], own_sem.at[2])
    own_rows.start()
    sq_out = []
    for k in send_order(n_out):
        c = remote(part.at[0], part.at[k], p_send.at[k], p_recv.at[k], to_out(k))
        c.start()
        sq_out.append(c)
    own_grad = pltpu.make_async_copy(rows_at(mine, in_me, rows), held.at[0], own_sem.at[3])
    own_grad.start()
    for c in sq_out:
        c.wait()
    total = jnp.sum(part[:n_out, 0:1, 0:1])
    acc[0] = jnp.full(acc.shape[1:], total, jnp.float32)
    sq_in = []
    for k in order:
        c = remote(acc.at[0], acc.at[k], q_send.at[k], q_recv.at[k], to_in(k))
        c.start()
        sq_in.append(c)
    attn_fwd = {}
    for k in order:
        c = remote(
            rows_at(asum, partner_to(in_me, k, n_in), a_rows), agot.at[k],
            h_send.at[k], h_recv.at[k], to_in(k),
        )
        c.start()
        attn_fwd[k] = c
    for k in rest:
        send_fwd(k)
    for c in sq_in:
        c.wait()
    total = jnp.sum(acc[:n_in, 0:1, 0:1])
    clip = 1.0 / jnp.sqrt(jnp.full((1, 1), total, jnp.float32) / numel + 1e-06)

    own_rows.wait()
    for c in state:
        c.wait()
    arow = row_chunk(a_rows)

    def update(k, source, got, back, refs, n_rows, n_cols, cc, rchunk):
        master, moment, second = refs

        def body(i, _):
            r = pl.ds(pl.multiple_of(i * rchunk, rchunk), rchunk)
            for c in range(n_cols // cc):
                cols = pl.ds(pl.multiple_of(source * n_cols + c * cc, 128), cc)
                here = slice(c * cc, (c + 1) * cc)
                g = got[k, r, here].astype(jnp.float32)
                a, b, d = adam_update(g, master[r, cols], moment[r, cols], second[r, cols], clip)
                master[r, cols] = a
                moment[r, cols] = b
                second[r, cols] = d
                back[k, r, here] = a.astype(jnp.bfloat16)
            return 0

        lax.fori_loop(0, n_rows // rchunk, body, 0)

    block_base = out_me * block_rows

    def attn_place(owner):
        return aw_o.at[pl.ds(pl.multiple_of(block_base + owner * a_rows, a_rows), a_rows)]

    attn_back = []
    attn_refs = (am_o, ao_o, as_o)
    for k in order + [0]:
        if k:
            attn_fwd[k].wait_recv()
        update(k, partner_from(in_me, k, n_in), agot, aback, attn_refs, a_rows, a_width, a_chunk, arow)
    for k in order:
        where = (out_me, partner_from(in_me, k, n_in))
        c = remote(aback.at[k], attn_place(in_me), r_send.at[k], r_recv.at[k], where)
        c.start()
        attn_back.append(c)
    attn_own = pltpu.make_async_copy(aback.at[0], attn_place(in_me), own_sem.at[4])
    attn_own.start()

    erow = row_chunk(rows)
    e_refs = (em_o, eo_o, es_o)
    back = []
    gather = []
    for k in arrival:
        if k:
            fwd[k].wait_recv()
        else:
            own_grad.wait()
        update(k, partner_from(in_me, k, n_in), held, held, e_refs, rows, width, chunk, erow)
        if k:
            where = (out_me, partner_from(in_me, k, n_in))
            c = remote(held.at[k], rows_at(ew_o, in_me, rows), s_send.at[k], s_recv.at[k], where)
            c.start()
            back.append(c)
        else:
            own_weight = pltpu.make_async_copy(held.at[0], rows_at(ew_o, in_me, rows), own_sem.at[5])
            own_weight.start()
    attn_own.wait()
    for c in attn_back:
        c.wait_recv()
    for k in send_order(n_out):
        mine_rows = rows_at(aw_o, out_me, block_rows)
        c = remote(mine_rows, mine_rows, t_send.at[k], t_recv.at[k], to_out(k))
        c.start()
        gather.append(c)

    for k in order:
        fwd[k].wait_send()
        attn_fwd[k].wait_send()
    for k in send_order(n_out):
        rep_copies[k].wait_send()
    for c in attn_back:
        c.wait_send()
    own_weight.wait()
    for c in gather:
        c.wait()
    for c in back:
        c.wait()


def put_kernel(*refs):
    count = (len(refs) - 1) // 2
    sem = refs[-1]
    copies = [
        pltpu.make_async_copy(refs[i], refs[count + i], sem.at[i]) for i in range(count)
    ]
    for c in copies:
        c.start()
    for c in copies:
        c.wait()


def local(n_out, n_in, eg, ag, em, eo, es, am, ao, as_):
    experts, e_rows, width = eg.shape
    eg = eg.reshape(experts * e_rows, width)
    ag = ag.reshape(ag.shape[1], ag.shape[2])
    numel = (em.shape[0] * em.shape[1] + am.shape[0] * am.shape[1]) * n_out * n_in
    rows = em.shape[0]
    a_rows = am.shape[0]
    a_width = ag.shape[1]
    block_rows = ag.shape[0] // n_out
    f32, bf16 = jnp.float32, jnp.bfloat16
    shapes = [(em.shape, f32)] * 3 + [(am.shape, f32)] * 3 + [(eg.shape, bf16), (ag.shape, bf16)]
    any_spec = pl.BlockSpec(memory_space=pl.ANY)
    vmem_spec = pl.BlockSpec(memory_space=pltpu.VMEM)
    dma = pltpu.SemaphoreType.DMA
    out = pl.pallas_call(
        functools.partial(step_kernel, n_out, n_in, float(numel)),
        out_shape=[pltpu.VMEM(s, d) for s, d in shapes],
        in_specs=[pl.BlockSpec(memory_space=pltpu.HBM)] * 8,
        out_specs=[vmem_spec] * 8,
        scratch_shapes=[
            pltpu.VMEM(eg.shape, bf16),
            pltpu.VMEM((n_in, rows, width), bf16),
            pltpu.VMEM((n_out, block_rows, a_width), bf16),
            pltpu.VMEM((block_rows, a_width), f32),
            pltpu.VMEM((n_in, a_rows, a_width), f32),
            pltpu.VMEM((n_in, a_rows, a_width), bf16),
            pltpu.VMEM((n_out, 8, 128), f32),
            pltpu.VMEM((n_in, 8, 128), f32),
            dma((6,)), dma((6,)),
            dma((n_in,)), dma((n_in,)),
            dma((n_out,)), dma((n_out,)),
            dma((n_in,)), dma((n_in,)),
            dma((n_out,)), dma((n_out,)),
            dma((n_in,)), dma((n_in,)),
            dma((n_in,)), dma((n_in,)),
            dma((n_in,)), dma((n_in,)),
            dma((n_out,)), dma((n_out,)),
        ],
        compiler_params=pltpu.CompilerParams(
            collective_id=0, has_side_effects=True, vmem_limit_bytes=30 * 1024 * 1024
        ),
    )(eg, ag, em, eo, es, am, ao, as_)
    moved = [x for i, x in enumerate(out) if i != 1]
    put = pl.pallas_call(
        put_kernel,
        out_shape=[jax.ShapeDtypeStruct(x.shape, x.dtype) for x in moved],
        in_specs=[vmem_spec] * 7,
        out_specs=[any_spec] * 7,
        scratch_shapes=[dma((7,))],
        compiler_params=pltpu.CompilerParams(vmem_limit_bytes=1024 * 1024),
    )(*moved)
    out = [put[0], out[1], *put[1:]]
    return (*out[:6], out[6].reshape(experts, e_rows, width), out[7])


def solution(mesh):
    grouped = P(("gx", "gy"), None)
    in_specs = (P("gx", None, "gy"), P("gx", None, "gy")) + (grouped,) * 6
    out_specs = (grouped,) * 6 + (P("gx", None, "gy"), P(None, "gy"))
    step = functools.partial(local, mesh.shape["gx"], mesh.shape["gy"])
    return jax.shard_map(step, mesh=mesh, in_specs=in_specs, out_specs=out_specs, check_vma=False)
```

profile of v0, /device:TPU:0, one launch (start us, length us, event | category | flops | bytes accessed | tf_op | source)
XLA Modules:
  0.0 211.8 jit_solution(18325894657257636590)
XLA Ops:
  0.6 200.1 %shard_map.143 = (f32[128,14336]{1,0:T(8,128)S(1)}, f32[128,14336]{1,0:T(8,128)S(1)}, f32[128,14336]{1,0:T(8,128)S(1)}, f32[64,4096]{1,0:T(8,128)S(1)}, f32[64,4...) custom-call(bf16[1024,1792]{1,0:T(8,128)(2,1)} %bitcast.3, ...), custom_call_target="tpu_custom_call" | custom-call | tf_op jit(solution)/shard_map/pallas_call | solution.py:311
  200.7 8.1 %shard_map.144 = (f32[128,14336]{1,0:T(8,128)}, f32[128,14336]{1,0:T(8,128)}, f32[64,4096]{1,0:T(8,128)}, f32[64,4096]{1,0:T(8,128)}, f32[64,4096]{1,0:T(8,128)}...) custom-call(f32[128,14336]{1,0:T(8,128)S(1)} %get-tuple-element.23.refs_0_, ...), custom_call_target="tpu_custom_call" | custom-call | tf_op jit(solution)/shard_map/pallas_call | solution.py:340
  208.8 3.1 %copy.17 = f32[128,14336]{1,0:T(8,128)} copy(f32[128,14336]{1,0:T(8,128)S(1)} %get-tuple-element.39) | data formatting | bytes 14680064
where the time goes:
time: 212 us
  Pallas kernels  208 us (98%)
  local copies, waits for them, and re-layouts  3.05 us (1%)
    pallas_call x1, Pallas kernels, local(): pl.pallas_call(functools.partial(step_kernel, n_out, n_in, float(numel)),...  200 us
    pallas_call x1, Pallas kernels, local(): pl.pallas_call(put_kernel, out_shape=[jax.ShapeDtypeStruct(x.shape, x.dty...  8.06 us

commit v1 on v0

--- a/solution.py
+++ b/solution.py
@@ -57,11 +57,27 @@
     return math.gcd(rows, 16)
 
 
+top = 2.0**15.5
+floor = 2.0**-15.5
+
+
+def encode(x):
+    square = x * x
+    fourth = square * square
+    eighth = jnp.where(jnp.abs(x) < floor, 0.0, fourth * fourth)
+    return jnp.where(x < 0.0, -eighth, eighth)
+
+
+def decode(y):
+    root = jnp.sqrt(jnp.sqrt(jnp.sqrt(jnp.abs(y))))
+    return jnp.where(y < 0.0, -root, root)
+
+
 def step_kernel(
     n_out, n_in, numel,
     eg, ag, em, eo, es, am, ao, as_,
     em_o, eo_o, es_o, am_o, ao_o, as_o, ew_o, aw_o,
-    mine, held, arep, asum, agot, aback, part, acc,
+    mine, held, arep, asum, acode, agot, part, acc,
     own_sem, state_sem, f_send, f_recv, g_send, g_recv, h_send, h_recv,
     p_send, p_recv, q_send, q_recv, r_send, r_recv, s_send, s_recv, t_send, t_recv,
 ):
@@ -152,6 +168,7 @@
     arc = row_chunk(block_rows)
 
     def sum_rows(i, carry):
+        squares, largest = carry
         r = pl.ds(pl.multiple_of(i * arc, arc), arc)
         for c in range(a_width // a_chunk):
             cols = slice(c * a_chunk, (c + 1) * a_chunk)
@@ -159,26 +176,40 @@
             for k in range(1, n_out):
                 x = x + arep[k, r, cols].astype(jnp.float32)
             asum[r, cols] = x
-            carry = carry + x * x
-        return carry
-
-    a_sq = lax.fori_loop(0, block_rows // arc, sum_rows, jnp.zeros((arc, a_chunk), jnp.float32))
+            squares = squares + x * x
+            largest = jnp.maximum(largest, jnp.abs(x))
+        return squares, largest
+
+    zeros = jnp.zeros((arc, a_chunk), jnp.float32)
+    a_sq, a_max = lax.fori_loop(0, block_rows // arc, sum_rows, (zeros, zeros))
     total = jnp.sum(e_sq) + jnp.sum(a_sq)
     part[0] = jnp.full(part.shape[1:], total, jnp.float32)
 
-    own_rows = pltpu.make_async_copy(rows_at(asum, in_me, a_rows), agot.at[0], own_sem.at[2])
+    sq_out = []
+    for k in send_order(n_out):
+        c = remote(part.at[0], part.at[k], p_send.at[k], p_recv.at[k], to_out(k))
+        c.start()
+        sq_out.append(c)
+    largest = jnp.maximum(jnp.max(a_max), 1e-30)
+    scale = jnp.full((1, 1), top, jnp.float32) / largest
+
+    def code_rows(i, _):
+        r = pl.ds(pl.multiple_of(i * arc, arc), arc)
+        for c in range(a_width // a_chunk):
+            cols = slice(c * a_chunk, (c + 1) * a_chunk)
+            acode[r, cols] = encode(asum[r, cols] * scale).astype(jnp.bfloat16)
+        return 0
+
+    lax.fori_loop(0, block_rows // arc, code_rows, 0)
+    own_rows = pltpu.make_async_copy(rows_at(acode, in_me, a_rows), agot.at[0], own_sem.at[2])
     own_rows.start()
-    sq_out = []
-    for k in send_order(n_out):
-        c = remote(part.at[0], part.at[k], p_send.at[k], p_recv.at[k], to_out(k))
-        c.start()
-        sq_out.append(c)
     own_grad = pltpu.make_async_copy(rows_at(mine, in_me, rows), held.at[0], own_sem.at[3])
     own_grad.start()
     for c in sq_out:
         c.wait()
     total = jnp.sum(part[:n_out, 0:1, 0:1])
-    acc[0] = jnp.full(acc.shape[1:], total, jnp.float32)
+    acc[0, 0:4] = jnp.full((4, acc.shape[2]), total, jnp.float32)
+    acc[0, 4:8] = jnp.full((4, acc.shape[2]), largest, jnp.float32)
     sq_in = []
     for k in order:
         c = remote(acc.at[0], acc.at[k], q_send.at[k], q_recv.at[k], to_in(k))
@@ -187,7 +218,7 @@
     attn_fwd = {}
     for k in order:
         c = remote(
-            rows_at(asum, partner_to(in_me, k, n_in), a_rows), agot.at[k],
+            rows_at(acode, partner_to(in_me, k, n_in), a_rows), agot.at[k],
             h_send.at[k], h_recv.at[k], to_in(k),
         )
         c.start()
@@ -204,7 +235,7 @@
         c.wait()
     arow = row_chunk(a_rows)
 
-    def update(k, source, got, back, refs, n_rows, n_cols, cc, rchunk):
+    def update(k, source, held, factor, load, refs, n_rows, n_cols, cc, rchunk):
         master, moment, second = refs
 
         def body(i, _):
@@ -212,12 +243,12 @@
             for c in range(n_cols // cc):
                 cols = pl.ds(pl.multiple_of(source * n_cols + c * cc, 128), cc)
                 here = slice(c * cc, (c + 1) * cc)
-                g = got[k, r, here].astype(jnp.float32)
-                a, b, d = adam_update(g, master[r, cols], moment[r, cols], second[r, cols], clip)
+                g = load(held[k, r, here].astype(jnp.float32))
+                a, b, d = adam_update(g, master[r, cols], moment[r, cols], second[r, cols], factor)
                 master[r, cols] = a
                 moment[r, cols] = b
                 second[r, cols] = d
-                back[k, r, here] = a.astype(jnp.bfloat16)
+                held[k, r, here] = a.astype(jnp.bfloat16)
             return 0
 
         lax.fori_loop(0, n_rows // rchunk, body, 0)
@@ -232,13 +263,17 @@
     for k in order + [0]:
         if k:
             attn_fwd[k].wait_recv()
-        update(k, partner_from(in_me, k, n_in), agot, aback, attn_refs, a_rows, a_width, a_chunk, arow)
+        factor = clip * (acc[k, 4:5, 0:1] / top)
+        update(
+            k, partner_from(in_me, k, n_in), agot, factor, decode, attn_refs,
+            a_rows, a_width, a_chunk, arow,
+        )
     for k in order:
         where = (out_me, partner_from(in_me, k, n_in))
-        c = remote(aback.at[k], attn_place(in_me), r_send.at[k], r_recv.at[k], where)
+        c = remote(agot.at[k], attn_place(in_me), r_send.at[k], r_recv.at[k], where)
         c.start()
         attn_back.append(c)
-    attn_own = pltpu.make_async_copy(aback.at[0], attn_place(in_me), own_sem.at[4])
+    attn_own = pltpu.make_async_copy(agot.at[0], attn_place(in_me), own_sem.at[4])
     attn_own.start()
 
     erow = row_chunk(rows)
@@ -250,7 +285,10 @@
             fwd[k].wait_recv()
         else:
             own_grad.wait()
-        update(k, partner_from(in_me, k, n_in), held, held, e_refs, rows, width, chunk, erow)
+        update(
+            k, partner_from(in_me, k, n_in), held, clip, lambda g: g, e_refs,
+            rows, width, chunk, erow,
+        )
         if k:
             where = (out_me, partner_from(in_me, k, n_in))
             c = remote(held.at[k], rows_at(ew_o, in_me, rows), s_send.at[k], s_recv.at[k], where)
@@ -318,7 +356,7 @@
             pltpu.VMEM((n_in, rows, width), bf16),
             pltpu.VMEM((n_out, block_rows, a_width), bf16),
             pltpu.VMEM((block_rows, a_width), f32),
-            pltpu.VMEM((n_in, a_rows, a_width), f32),
+            pltpu.VMEM((block_rows, a_width), bf16),
             pltpu.VMEM((n_in, a_rows, a_width), bf16),
             pltpu.VMEM((n_out, 8, 128), f32),
             pltpu.VMEM((n_in, 8, 128), f32),
@@ -333,19 +371,17 @@
             dma((n_out,)), dma((n_out,)),
         ],
         compiler_params=pltpu.CompilerParams(
-            collective_id=0, has_side_effects=True, vmem_limit_bytes=30 * 1024 * 1024
+            collective_id=0, has_side_effects=True, vmem_limit_bytes=26 * 1024 * 1024
         ),
     )(eg, ag, em, eo, es, am, ao, as_)
-    moved = [x for i, x in enumerate(out) if i != 1]
-    put = pl.pallas_call(
+    out = pl.pallas_call(
         put_kernel,
-        out_shape=[jax.ShapeDtypeStruct(x.shape, x.dtype) for x in moved],
-        in_specs=[vmem_spec] * 7,
-        out_specs=[any_spec] * 7,
-        scratch_shapes=[dma((7,))],
+        out_shape=[jax.ShapeDtypeStruct(x.shape, x.dtype) for x in out],
+        in_specs=[vmem_spec] * 8,
+        out_specs=[any_spec] * 8,
+        scratch_shapes=[dma((8,))],
         compiler_params=pltpu.CompilerParams(vmem_limit_bytes=1024 * 1024),
-    )(*moved)
-    out = [put[0], out[1], *put[1:]]
+    )(*out)
     return (*out[:6], out[6].reshape(experts, e_rows, width), out[7])
 
 

time: 212 us -> 200 us (0.943)
  Pallas kernels: 208 us -> 199 us
  local copies, waits for them, and re-layouts: 3.05 us -> 0 us
    pallas_call x1, Pallas kernels: 200 us -> 189 us  [local(): pl.pallas_call(functools.partial(step_kernel, n_out, n_in, float(numel)),...]
    unnamed x1 -> x0, local copies, waits for them, and re-layouts: 3.05 us -> none
    pallas_call x1, Pallas kernels: 8.06 us -> 10.3 us  [local(): pl.pallas_call(put_kernel, out_shape=[jax.ShapeDtypeStruct(x.shape, x.dty...]
where the time goes in v1:
time: 200 us
  Pallas kernels  199 us (100%)
    pallas_call x1, Pallas kernels, local(): pl.pallas_call(functools.partial(step_kernel, n_out, n_in, float(numel)),...  189 us
    pallas_call x1, Pallas kernels, local(): pl.pallas_call(put_kernel, out_shape=[jax.ShapeDtypeStruct(x.shape, x.dty...  10.3 us

profile of v1, /device:TPU:0, one launch (start us, length us, event | category | flops | bytes accessed | tf_op | source)
XLA Modules:
  0.0 199.7 jit_solution(10547845785801403162)
XLA Ops:
  0.6 188.8 %shard_map.143 = (f32[128,14336]{1,0:T(8,128)S(1)}, f32[128,14336]{1,0:T(8,128)S(1)}, f32[128,14336]{1,0:T(8,128)S(1)}, f32[64,4096]{1,0:T(8,128)S(1)}, f32[64,4...) custom-call(bf16[1024,1792]{1,0:T(8,128)(2,1)} %bitcast.3, ...), custom_call_target="tpu_custom_call" | custom-call | tf_op jit(solution)/shard_map/pallas_call | solution.py:349
  189.5 10.3 %shard_map.144 = (f32[128,14336]{1,0:T(8,128)}, f32[128,14336]{1,0:T(8,128)}, f32[128,14336]{1,0:T(8,128)}, f32[64,4096]{1,0:T(8,128)}, f32[64,4096]{1,0:T(8,128...) custom-call(f32[128,14336]{1,0:T(8,128)S(1)} %get-tuple-element.24.refs_0_, ...), custom_call_target="tpu_custom_call" | custom-call | tf_op jit(solution)/shard_map/pallas_call | solution.py:377

commit v2 on v1

--- a/solution.py
+++ b/solution.py
@@ -57,6 +57,18 @@
     return math.gcd(rows, 16)
 
 
+def partner_of(me, k, n):
+    return (me + k) % n if n & (n - 1) else me ^ k
+
+
+def far_blocks(n):
+    return [n - 2]
+
+
+def kept_rows(rows):
+    return max(rows * 6 // 8 // 16 * 16, 16) if rows > 16 else rows // 2
+
+
 top = 2.0**15.5
 floor = 2.0**-15.5
 
@@ -76,7 +88,7 @@
 def step_kernel(
     n_out, n_in, numel,
     eg, ag, em, eo, es, am, ao, as_,
-    em_o, eo_o, es_o, am_o, ao_o, as_o, ew_o, aw_o,
+    em_o, eo_o, es_o, am_o, ao_o, as_o, ew_o, aw_o, left,
     mine, held, arep, asum, acode, agot, part, acc,
     own_sem, state_sem, f_send, f_recv, g_send, g_recv, h_send, h_recv,
     p_send, p_recv, q_send, q_recv, r_send, r_recv, s_send, s_recv, t_send, t_recv,
@@ -291,7 +303,13 @@
         )
         if k:
             where = (out_me, partner_from(in_me, k, n_in))
-            c = remote(held.at[k], rows_at(ew_o, in_me, rows), s_send.at[k], s_recv.at[k], where)
+            sent = rows
+            if k in far_blocks(n_in):
+                keep = kept_rows(rows)
+                sent = rows - keep
+                left[far_blocks(n_in).index(k)] = held[k, sent:rows]
+            place = pl.ds(pl.multiple_of(in_me * rows, rows), sent)
+            c = remote(held.at[k, 0:sent], ew_o.at[place], s_send.at[k], s_recv.at[k], where)
             c.start()
             back.append(c)
         else:
@@ -332,6 +350,22 @@
         c.wait()
 
 
+def last_kernel(n_in, rows, *refs):
+    count = len(refs) - 3
+    out, sem = refs[-2:]
+    in_me = lax.axis_index("gy")
+    copies = []
+    for i, k in enumerate(far_blocks(n_in)):
+        keep = refs[1 + i].shape[0]
+        start = partner_to(in_me, k, n_in) * rows + (rows - keep)
+        place = pl.ds(pl.multiple_of(start, math.gcd(rows, keep)), keep)
+        copies.append(pltpu.make_async_copy(refs[1 + i], out.at[place], sem.at[i]))
+    for c in copies:
+        c.start()
+    for c in copies:
+        c.wait()
+
+
 def local(n_out, n_in, eg, ag, em, eo, es, am, ao, as_):
     experts, e_rows, width = eg.shape
     eg = eg.reshape(experts * e_rows, width)
@@ -343,6 +377,8 @@
     block_rows = ag.shape[0] // n_out
     f32, bf16 = jnp.float32, jnp.bfloat16
     shapes = [(em.shape, f32)] * 3 + [(am.shape, f32)] * 3 + [(eg.shape, bf16), (ag.shape, bf16)]
+    far = far_blocks(n_in)
+    shapes += [((len(far), kept_rows(rows), width), bf16)]
     any_spec = pl.BlockSpec(memory_space=pl.ANY)
     vmem_spec = pl.BlockSpec(memory_space=pltpu.VMEM)
     dma = pltpu.SemaphoreType.DMA
@@ -350,7 +386,7 @@
         functools.partial(step_kernel, n_out, n_in, float(numel)),
         out_shape=[pltpu.VMEM(s, d) for s, d in shapes],
         in_specs=[pl.BlockSpec(memory_space=pltpu.HBM)] * 8,
-        out_specs=[vmem_spec] * 8,
+        out_specs=[vmem_spec] * 9,
         scratch_shapes=[
             pltpu.VMEM(eg.shape, bf16),
             pltpu.VMEM((n_in, rows, width), bf16),
@@ -374,6 +410,12 @@
             collective_id=0, has_side_effects=True, vmem_limit_bytes=26 * 1024 * 1024
         ),
     )(eg, ag, em, eo, es, am, ao, as_)
+    *out, left = out
+    came = [
+        lax.ppermute(left[i], "gy", [(j, partner_of(j, k, n_in)) for j in range(n_in)])
+        for i, k in enumerate(far)
+    ]
+    moved = sum(x.size * x.dtype.itemsize for x in out)
     out = pl.pallas_call(
         put_kernel,
         out_shape=[jax.ShapeDtypeStruct(x.shape, x.dtype) for x in out],
@@ -381,7 +423,18 @@
         out_specs=[any_spec] * 8,
         scratch_shapes=[dma((8,))],
         compiler_params=pltpu.CompilerParams(vmem_limit_bytes=1024 * 1024),
+        cost_estimate=pl.CostEstimate(flops=0, bytes_accessed=2 * moved, transcendentals=0),
     )(*out)
+    out = list(out)
+    out[6] = pl.pallas_call(
+        functools.partial(last_kernel, n_in, rows),
+        out_shape=jax.ShapeDtypeStruct(out[6].shape, bf16),
+        in_specs=[any_spec] + [vmem_spec] * len(far),
+        out_specs=any_spec,
+        scratch_shapes=[dma((len(far),))],
+        input_output_aliases={0: 0},
+        compiler_params=pltpu.CompilerParams(vmem_limit_bytes=1024 * 1024),
+    )(out[6], *came)
     return (*out[:6], out[6].reshape(experts, e_rows, width), out[7])
 
 

time: 200 us -> 189 us (0.945)
  Pallas kernels: 199 us -> 185 us
  starting transfers between devices: 0 us -> 2.11 us
    pallas_call x1, Pallas kernels: 189 us -> 174 us  [local(): pl.pallas_call(functools.partial(step_kernel, n_out, n_in, float(numel)),...]
    ppermute x0 -> x1, starting transfers between devices: none -> 2.11 us  [local(): lax.ppermute(left[i], 'gy', [(j, partner_of(j, k, n_in)) for j in range(n...]
  transfers between devices with their start and end apart: 0 -> 1, of which waited for: 0 -> 0; matrix products, arithmetic and copies ran while one was open for 0% -> 0% of each run, Pallas kernels for 0% -> 5%
where the time goes in v2:
time: 189 us; the launch traced here: 188 us
  Pallas kernels  185 us (98%)
  starting transfers between devices  2.11 us (1%)
    pallas_call x1, Pallas kernels, local(): pl.pallas_call(functools.partial(step_kernel, n_out, n_in, float(numel)),...  174 us
    pallas_call x1, Pallas kernels, local(): pl.pallas_call(put_kernel, out_shape=[jax.ShapeDtypeStruct(x.shape, x.dty...  10.3 us
  transfers between devices with their start and end apart: 1, of which 0 were waited for; matrix products, arithmetic and copies ran while one was open for 0% of the time, Pallas kernels for 5%

profile of v2, /device:TPU:0, one launch (start us, length us, event | category | flops | bytes accessed | tf_op | source)
XLA Modules:
  0.0 187.9 jit_solution(16043443461601718958)
XLA Ops:
  0.6 174.1 %shard_map.143 = (f32[128,14336]{1,0:T(8,128)S(1)}, f32[128,14336]{1,0:T(8,128)S(1)}, f32[128,14336]{1,0:T(8,128)S(1)}, f32[64,4096]{1,0:T(8,128)S(1)}, f32[64,4...) custom-call(bf16[1024,1792]{1,0:T(8,128)(2,1)} %bitcast.6, ...), custom_call_target="tpu_custom_call" | custom-call | tf_op jit(solution)/shard_map/pallas_call | solution.py:385
  174.7 2.1 %collective-permute-start = (bf16[96,1792]{1,0:T(8,128)(2,1)S(1)}, bf16[96,1792]{1,0:T(8,128)(2,1)S(1)}, u32[]{:S(2)}, u32[]{:S(2)}) collective-permute-start(bf16[96,1792]{1,0:T(8,128)(2,1)S(1)} %bitcast.4), channel_id=1, source_target_pairs={{0,6},{1,7},{2,4},{3,5},{4,2},{5,3},{6,0},{7,1},{8,14},{9,15},{10,... | collective-permute-start | bytes 1032200 | tf_op jit(solution)/shard_map/ppermute | solution.py:415
  176.8 10.3 %shard_map.144 = (f32[128,14336]{1,0:T(8,128)}, f32[128,14336]{1,0:T(8,128)}, f32[128,14336]{1,0:T(8,128)}, f32[64,4096]{1,0:T(8,128)}, f32[64,4096]{1,0:T(8,128...) custom-call(f32[128,14336]{1,0:T(8,128)S(1)} %get-tuple-element.25.refs_0_, ...), custom_call_target="tpu_custom_call" | custom-call | bytes 61865984 | tf_op jit(solution)/shard_map/pallas_call | solution.py:419
  187.1 0.0 collective-permute-done.refs_1_
  187.1 0.8 shard_map.145
Async XLA Ops:
  174.7 12.4 %collective-permute-start = (bf16[96,1792]{1,0:T(8,128)(2,1)S(1)}, bf16[96,1792]{1,0:T(8,128)(2,1)S(1)}, u32[]{:S(2)}, u32[]{:S(2)}) collective-permute-start(bf16[96,1792]{1,0:T(8,128)(2,1)S(1)} %bitcast.4), channel_id=1, source_target_pairs={{0,6},{1,7},{2,4},{3,5},{4,2},{5,3},{6,0},{7,1},{8,14},{9,15},{10,... | collective-permute-start | bytes 1032200 | tf_op jit(solution)/shard_map/ppermute | solution.py:415

commit v3 on v2

--- a/solution.py
+++ b/solution.py
@@ -66,7 +66,7 @@
 
 
 def kept_rows(rows):
-    return max(rows * 6 // 8 // 16 * 16, 16) if rows > 16 else rows // 2
+    return max(rows * 5 // 8 // 16 * 16, 16) if rows > 16 else rows // 2
 
 
 top = 2.0**15.5
@@ -90,7 +90,7 @@
     eg, ag, em, eo, es, am, ao, as_,
     em_o, eo_o, es_o, am_o, ao_o, as_o, ew_o, aw_o, left,
     mine, held, arep, asum, acode, agot, part, acc,
-    own_sem, state_sem, f_send, f_recv, g_send, g_recv, h_send, h_recv,
+    ready, own_sem, load_sem, state_sem, f_send, f_recv, g_send, g_recv, h_send, h_recv,
     p_send, p_recv, q_send, q_recv, r_send, r_recv, s_send, s_recv, t_send, t_recv,
 ):
     out_me = lax.axis_index("gx")
@@ -115,16 +115,85 @@
         return ref.at[pl.ds(pl.multiple_of(index * count, count), count)]
 
     barrier = pltpu.get_barrier_semaphore()
-    for k in range(1, n_in):
-        pl.semaphore_signal(barrier, inc=1, device_id=to_in(k), device_id_type=MESH)
-    for k in range(1, n_out):
-        pl.semaphore_signal(barrier, inc=1, device_id=to_out(k), device_id_type=MESH)
-
-    load_grad = pltpu.make_async_copy(eg, mine, own_sem.at[0])
-    load_grad.start()
+
+    def signal(sem, where):
+        pl.semaphore_signal(sem, inc=1, device_id=where, device_id_type=MESH)
+
+    quarter = n_in // 4
+    staged = quarter > 0 and not n_in & (n_in - 1)
+    middle = outer = None
+    if staged:
+        middle = lax.rem(in_me // quarter, 2) != in_me // (2 * quarter)
+        outer = jnp.logical_not(middle)
+        for k in range(3 * quarter, n_in):
+            signal(barrier, to_in(k))
+
+        @pl.when(middle)
+        def _():
+            for k in range(quarter, 3 * quarter):
+                signal(barrier, to_in(k))
+
+        @pl.when(outer)
+        def _():
+            for k in range(1, quarter):
+                signal(barrier, to_in(k))
+            for k in range(1, n_out):
+                signal(barrier, to_out(k))
+    else:
+        for k in range(1, n_in):
+            signal(barrier, to_in(k))
+        for k in range(1, n_out):
+            signal(barrier, to_out(k))
+
+    order = send_order(n_in)
+    far, near = order[: n_in // 2], order[n_in // 2 :]
+    first = far[: n_in // 4] + near[:1]
+    rest = near[1:] + far[n_in // 4 :]
+    arrival = first + near[1:] + [0] + far[n_in // 4 :]
+
+    def block_of(ref, k):
+        return rows_at(ref, partner_to(in_me, k, n_in), rows)
+
+    load = {}
+    for k in first + rest + [0]:
+        load[k] = pltpu.make_async_copy(block_of(eg, k), block_of(mine, k), load_sem.at[k])
+        load[k].start()
     load_rep = pltpu.make_async_copy(rows_at(ag, out_me, block_rows), arep.at[0], own_sem.at[1])
     load_rep.start()
-    pl.semaphore_wait(barrier, n_in - 1 + n_out - 1)
+    everyone = n_in - 1 + n_out - 1
+    if staged:
+        @pl.when(middle)
+        def _():
+            pl.semaphore_wait(barrier, quarter)
+
+        @pl.when(outer)
+        def _():
+            pl.semaphore_wait(barrier, everyone)
+    else:
+        pl.semaphore_wait(barrier, everyone)
+
+    fwd = {}
+
+    def send_fwd(k):
+        c = remote(block_of(mine, k), held.at[k], f_send.at[k], f_recv.at[k], to_in(k))
+        c.start()
+        fwd[k] = c
+
+    for k in far[:quarter]:
+        load[k].wait()
+        send_fwd(k)
+    if staged:
+        @pl.when(outer)
+        def _():
+            for k in range(1, n_out):
+                signal(ready, to_out(k))
+            if n_out > 1:
+                pl.semaphore_wait(ready, n_out - 1)
+            signal(ready, to_in(quarter))
+
+        @pl.when(middle)
+        def _():
+            pl.semaphore_wait(ready, 1)
 
     rep_copies = {}
     for k in send_order(n_out):
@@ -134,22 +203,8 @@
         )
         c.start()
         rep_copies[k] = c
-    order = send_order(n_in)
-    far, near = order[: n_in // 2], order[n_in // 2 :]
-    first = far[: n_in // 4] + near[:1]
-    rest = near[1:] + far[n_in // 4 :]
-    arrival = first + near[1:] + [0] + far[n_in // 4 :]
-    fwd = {}
-
-    def send_fwd(k):
-        c = remote(
-            rows_at(eg, partner_to(in_me, k, n_in), rows), held.at[k],
-            f_send.at[k], f_recv.at[k], to_in(k),
-        )
-        c.start()
-        fwd[k] = c
-
-    for k in first:
+    for k in near[:1]:
+        load[k].wait()
         send_fwd(k)
 
     state = []
@@ -160,7 +215,8 @@
         c.start()
         state.append(c)
 
-    load_grad.wait()
+    for k in rest + [0]:
+        load[k].wait()
     chunk = col_chunk(width)
     rc = row_chunk(mine.shape[0])
 
@@ -305,16 +361,19 @@
             where = (out_me, partner_from(in_me, k, n_in))
             sent = rows
             if k in far_blocks(n_in):
-                keep = kept_rows(rows)
-                sent = rows - keep
+                sent = rows - kept_rows(rows)
                 left[far_blocks(n_in).index(k)] = held[k, sent:rows]
             place = pl.ds(pl.multiple_of(in_me * rows, rows), sent)
             c = remote(held.at[k, 0:sent], ew_o.at[place], s_send.at[k], s_recv.at[k], where)
-            c.start()
+            if sent == rows:
+                c.start()
             back.append(c)
         else:
             own_weight = pltpu.make_async_copy(held.at[0], rows_at(ew_o, in_me, rows), own_sem.at[5])
             own_weight.start()
+    for k, c in zip([k for k in arrival if k], back):
+        if k in far_blocks(n_in):
+            c.start()
     attn_own.wait()
     for c in attn_back:
         c.wait_recv()
@@ -396,7 +455,8 @@
             pltpu.VMEM((n_in, a_rows, a_width), bf16),
             pltpu.VMEM((n_out, 8, 128), f32),
             pltpu.VMEM((n_in, 8, 128), f32),
-            dma((6,)), dma((6,)),
+            pltpu.SemaphoreType.REGULAR,
+            dma((6,)), dma((n_in,)), dma((6,)),
             dma((n_in,)), dma((n_in,)),
             dma((n_out,)), dma((n_out,)),
             dma((n_in,)), dma((n_in,)),

time: 189 us -> 187 us (0.989)
  Pallas kernels: 185 us -> 183 us
  transfers between devices with their start and end apart: 1 -> 1, of which waited for: 0 -> 0; matrix products, arithmetic and copies ran while one was open for 0% -> 0% of each run, Pallas kernels for 5% -> 6%
where the time goes in v3:
time: 187 us; the launch traced here: 186 us
  Pallas kernels  183 us (98%)
  starting transfers between devices  1.92 us (1%)
    pallas_call x1, Pallas kernels, local(): pl.pallas_call(functools.partial(step_kernel, n_out, n_in, float(numel)),...  172 us
    pallas_call x1, Pallas kernels, local(): pl.pallas_call(put_kernel, out_shape=[jax.ShapeDtypeStruct(x.shape, x.dty...  10.3 us
  transfers between devices with their start and end apart: 1, of which 0 were waited for; matrix products, arithmetic and copies ran while one was open for 0% of the time, Pallas kernels for 6%

profile of v3, /device:TPU:0, one launch (start us, length us, event | category | flops | bytes accessed | tf_op | source)
XLA Modules:
  0.0 186.0 jit_solution(14062909754741767867)
XLA Ops:
  0.6 172.4 %shard_map.143 = (f32[128,14336]{1,0:T(8,128)S(1)}, f32[128,14336]{1,0:T(8,128)S(1)}, f32[128,14336]{1,0:T(8,128)S(1)}, f32[64,4096]{1,0:T(8,128)S(1)}, f32[64,4...) custom-call(bf16[1024,1792]{1,0:T(8,128)(2,1)} %bitcast.6, ...), custom_call_target="tpu_custom_call" | custom-call | tf_op jit(solution)/shard_map/pallas_call | solution.py:444
  173.0 1.9 %collective-permute-start = (bf16[80,1792]{1,0:T(8,128)(2,1)S(1)}, bf16[80,1792]{1,0:T(8,128)(2,1)S(1)}, u32[]{:S(2)}, u32[]{:S(2)}) collective-permute-start(bf16[80,1792]{1,0:T(8,128)(2,1)S(1)} %bitcast.4), channel_id=1, source_target_pairs={{0,6},{1,7},{2,4},{3,5},{4,2},{5,3},{6,0},{7,1},{8,14},{9,15},{10,... | collective-permute-start | bytes 860168 | tf_op jit(solution)/shard_map/ppermute | solution.py:475
  174.9 10.3 %shard_map.144 = (f32[128,14336]{1,0:T(8,128)}, f32[128,14336]{1,0:T(8,128)}, f32[128,14336]{1,0:T(8,128)}, f32[64,4096]{1,0:T(8,128)}, f32[64,4096]{1,0:T(8,128...) custom-call(f32[128,14336]{1,0:T(8,128)S(1)} %get-tuple-element.25.refs_0_, ...), custom_call_target="tpu_custom_call" | custom-call | bytes 61865984 | tf_op jit(solution)/shard_map/pallas_call | solution.py:479
  185.2 0.0 collective-permute-done.refs_1_
  185.2 0.7 shard_map.145
Async XLA Ops:
  173.0 12.2 %collective-permute-start = (bf16[80,1792]{1,0:T(8,128)(2,1)S(1)}, bf16[80,1792]{1,0:T(8,128)(2,1)S(1)}, u32[]{:S(2)}, u32[]{:S(2)}) collective-permute-start(bf16[80,1792]{1,0:T(8,128)(2,1)S(1)} %bitcast.4), channel_id=1, source_target_pairs={{0,6},{1,7},{2,4},{3,5},{4,2},{5,3},{6,0},{7,1},{8,14},{9,15},{10,... | collective-permute-start | bytes 860168 | tf_op jit(solution)/shard_map/ppermute | solution.py:475

commit v4 on v3

--- a/solution.py
+++ b/solution.py
@@ -65,8 +65,12 @@
     return [n - 2]
 
 
+def late_rows(rows):
+    return math.gcd(rows // 4, 32)
+
+
 def kept_rows(rows):
-    return max(rows * 5 // 8 // 16 * 16, 16) if rows > 16 else rows // 2
+    return max(rows * 6 // 8 // 16 * 16, 16) if rows > 16 else rows // 2
 
 
 top = 2.0**15.5
@@ -90,7 +94,7 @@
     eg, ag, em, eo, es, am, ao, as_,
     em_o, eo_o, es_o, am_o, ao_o, as_o, ew_o, aw_o, left,
     mine, held, arep, asum, acode, agot, part, acc,
-    ready, own_sem, load_sem, state_sem, f_send, f_recv, g_send, g_recv, h_send, h_recv,
+    ready, late_sem, own_sem, load_sem, state_sem, f_send, f_recv, g_send, g_recv, h_send, h_recv,
     p_send, p_recv, q_send, q_recv, r_send, r_recv, s_send, s_recv, t_send, t_recv,
 ):
     out_me = lax.axis_index("gx")
@@ -363,9 +367,15 @@
             if k in far_blocks(n_in):
                 sent = rows - kept_rows(rows)
                 left[far_blocks(n_in).index(k)] = held[k, sent:rows]
+            elif k == n_in - 1:
+                sent = rows - late_rows(rows)
+                place = pl.ds(pl.multiple_of(in_me * rows + sent, math.gcd(rows, sent)), rows - sent)
+                late = remote(
+                    held.at[k, sent:rows], ew_o.at[place], late_sem.at[0], late_sem.at[1], where
+                )
             place = pl.ds(pl.multiple_of(in_me * rows, rows), sent)
             c = remote(held.at[k, 0:sent], ew_o.at[place], s_send.at[k], s_recv.at[k], where)
-            if sent == rows:
+            if k not in far_blocks(n_in):
                 c.start()
             back.append(c)
         else:
@@ -374,6 +384,8 @@
     for k, c in zip([k for k in arrival if k], back):
         if k in far_blocks(n_in):
             c.start()
+    late.start()
+    back.append(late)
     attn_own.wait()
     for c in attn_back:
         c.wait_recv()
@@ -455,7 +467,7 @@
             pltpu.VMEM((n_in, a_rows, a_width), bf16),
             pltpu.VMEM((n_out, 8, 128), f32),
             pltpu.VMEM((n_in, 8, 128), f32),
-            pltpu.SemaphoreType.REGULAR,
+            pltpu.SemaphoreType.REGULAR, dma((2,)),
             dma((6,)), dma((n_in,)), dma((6,)),
             dma((n_in,)), dma((n_in,)),
             dma((n_out,)), dma((n_out,)),

time: 187 us -> 186 us (level); the launches traced: 186 us -> 182 us
  Pallas kernels: 183 us -> 180 us
    pallas_call x1, Pallas kernels: 172 us -> 169 us  [local(): pl.pallas_call(functools.partial(step_kernel, n_out, n_in, float(numel)),...]
where the time goes in v4:
time: 186 us; the launch traced here: 182 us
  Pallas kernels  180 us (97%)
  starting transfers between devices  1.92 us (1%)
    pallas_call x1, Pallas kernels, local(): pl.pallas_call(functools.partial(step_kernel, n_out, n_in, float(numel)),...  169 us
    pallas_call x1, Pallas kernels, local(): pl.pallas_call(put_kernel, out_shape=[jax.ShapeDtypeStruct(x.shape, x.dty...  10.3 us
  transfers between devices with their start and end apart: 1, of which 0 were waited for; matrix products, arithmetic and copies ran while one was open for 0% of the time, Pallas kernels for 6%

profile of v4, /device:TPU:0, one launch (start us, length us, event | category | flops | bytes accessed | tf_op | source)
XLA Modules:
  0.0 182.3 jit_solution(11888391037109274832)
XLA Ops:
  0.6 168.7 %shard_map.143 = (f32[128,14336]{1,0:T(8,128)S(1)}, f32[128,14336]{1,0:T(8,128)S(1)}, f32[128,14336]{1,0:T(8,128)S(1)}, f32[64,4096]{1,0:T(8,128)S(1)}, f32[64,4...) custom-call(bf16[1024,1792]{1,0:T(8,128)(2,1)} %bitcast.6, ...), custom_call_target="tpu_custom_call" | custom-call | tf_op jit(solution)/shard_map/pallas_call | solution.py:456
  169.4 1.9 %collective-permute-start = (bf16[96,1792]{1,0:T(8,128)(2,1)S(1)}, bf16[96,1792]{1,0:T(8,128)(2,1)S(1)}, u32[]{:S(2)}, u32[]{:S(2)}) collective-permute-start(bf16[96,1792]{1,0:T(8,128)(2,1)S(1)} %bitcast.4), channel_id=1, source_target_pairs={{0,6},{1,7},{2,4},{3,5},{4,2},{5,3},{6,0},{7,1},{8,14},{9,15},{10,... | collective-permute-start | bytes 1032200 | tf_op jit(solution)/shard_map/ppermute | solution.py:487
  171.3 10.3 %shard_map.144 = (f32[128,14336]{1,0:T(8,128)}, f32[128,14336]{1,0:T(8,128)}, f32[128,14336]{1,0:T(8,128)}, f32[64,4096]{1,0:T(8,128)}, f32[64,4096]{1,0:T(8,128...) custom-call(f32[128,14336]{1,0:T(8,128)S(1)} %get-tuple-element.25.refs_0_, ...), custom_call_target="tpu_custom_call" | custom-call | bytes 61865984 | tf_op jit(solution)/shard_map/pallas_call | solution.py:491
  181.5 0.0 collective-permute-done.refs_1_
  181.6 0.8 shard_map.145
Async XLA Ops:
  169.4 12.2 %collective-permute-start = (bf16[96,1792]{1,0:T(8,128)(2,1)S(1)}, bf16[96,1792]{1,0:T(8,128)(2,1)S(1)}, u32[]{:S(2)}, u32[]{:S(2)}) collective-permute-start(bf16[96,1792]{1,0:T(8,128)(2,1)S(1)} %bitcast.4), channel_id=1, source_target_pairs={{0,6},{1,7},{2,4},{3,5},{4,2},{5,3},{6,0},{7,1},{8,14},{9,15},{10,... | collective-permute-start | bytes 1032200 | tf_op jit(solution)/shard_map/ppermute | solution.py:487
